TPU v7x, 32 devices: a whole 2x2x4 slice. The times are simulated.
32 devices in a mesh: fsdp: 8 (over y, x, core), tp: 4 (over z).
Axes of the slice: x: 2, y: 2, z: 4, core: 2. Of those that a mesh axis runs over, the one named last changes fastest.
Arguments:
- emb: bfloat16 [8192, 1536], P(('fsdp', 'tp')), may hold values from -0.5 to 0.5
- segment_ids: int32 [16, 512], P('fsdp'), may hold values from 0 to 3, never falling along the last dimension, each value on 1 to 256 neighbouring positions
- routes: int32 [8192, 8], P('fsdp'), may hold values from 0 to 39, all different within a row; in each aligned block of 1024 rows (0 to 1023, 1024 to 2047, ...) at most 408 rows name the same one
- norm1_gain: bfloat16 [1536], replicated, may hold values from 0.5 to 1.5
- w_query: bfloat16 [1536, 1536], P('fsdp', 'tp'), may hold values from -0.625 to 0.625
- w_key: bfloat16 [1536, 512], P('fsdp', 'tp'), may hold values from -0.625 to 0.625
- w_value: bfloat16 [1536, 512], P('fsdp', 'tp'), may hold values from -0.15625 to 0.15625
- w_out: bfloat16 [1536, 1536], P('fsdp', 'tp'), may hold values from -1.25 to 1.25
- norm2_gain: bfloat16 [1536], replicated, may hold values from 0.5 to 1.5
- w_router: bfloat16 [1536, 40], P('fsdp'), may hold values from -0.15625 to 0.15625
- w_gate: bfloat16 [40, 1536, 512], P('tp', 'fsdp'), may hold values from -0.15625 to 0.15625
- w_up: bfloat16 [40, 1536, 512], P('tp', 'fsdp'), may hold values from -0.15625 to 0.15625
- w_down: bfloat16 [40, 1536, 512], P('tp', 'fsdp'), may hold values from -3 to 3
- cotangent: bfloat16 [8192, 1536], P(('fsdp', 'tp')), may hold values from -6 to 6
Outputs:
- out: bfloat16 [8192, 1536], P(('fsdp', 'tp'))
- grad_emb: float32 [8192, 1536], P(('fsdp', 'tp'))
- grad_norm1_gain: float32 [1536], replicated
- grad_w_query: float32 [1536, 1536], P('fsdp', 'tp')
- grad_w_key: float32 [1536, 512], P('fsdp', 'tp')
- grad_w_value: float32 [1536, 512], P('fsdp', 'tp')
- grad_w_out: float32 [1536, 1536], P('fsdp', 'tp')
- grad_norm2_gain: float32 [1536], replicated
- grad_w_router: float32 [1536, 40], P('fsdp')
- grad_w_gate: float32 [40, 1536, 512], P('tp', 'fsdp')
- grad_w_up: float32 [40, 1536, 512], P('tp', 'fsdp')
- grad_w_down: float32 [40, 1536, 512], P('tp', 'fsdp')
Inputs may be any that keep to these rules, and one draw needn't show every extreme that they name: `routes`: in each aligned block of 1024 rows no expert is named by more than 408 rows, a bound that some block reaches. `segment_ids`: along a sequence the numbers never fall; a document spans at most 256 tokens, and one spans exactly 256.
All inputs are finite; a program needn't handle non-finite values.
Results may differ from a plain program's by a relative error of at most 0.015.
Values may be sent and summed in bfloat16 or wider, within the bound.
A program may use at most 384 MiB of HBM per device.

v0:
```python
import jax
import jax.numpy as jnp
from jax import lax
from jax.sharding import PartitionSpec as P

HEAD_DIM = 64
SEQ = 512
emb_scale = 12.0
resid_scale = 0.22
attn_scale = 0.015625
norm_eps = 1e-06
rope_base = 10000.0
masked_value = -1e30


def contract_last(left_op, right_op):
    return lax.dot_general(
        left_op, right_op, (((1,), (1,)), ((), ())), preferred_element_type=jnp.float32
    )


def contract_first(left_op, right_op):
    return lax.dot_general(
        left_op, right_op, (((0,), (0,)), ((), ())), preferred_element_type=jnp.float32
    )


def rms_forward(values, gain_vec):
    inverse = lax.rsqrt(jnp.mean(values * values, axis=-1, keepdims=True) + norm_eps)
    return (values * inverse * gain_vec, inverse)


def rms_backward(incoming, values, inverse, gain_vec):
    scaled = values * inverse
    gain_grad = jnp.sum(incoming * scaled, axis=0)
    weighted = incoming * gain_vec
    row_inner = jnp.mean(weighted * scaled, axis=-1, keepdims=True)
    return (inverse * (weighted - scaled * row_inner), gain_grad)


def rotary_tables(row_count, head_width):
    half_width = head_width // 2
    positions = (jnp.arange(row_count) % SEQ).astype(jnp.float32)
    frequency = rope_base ** (-jnp.arange(half_width).astype(jnp.float32) * 2.0 / head_width)
    angles = positions[:, None] * frequency[None, :]
    return (jnp.cos(angles)[:, None, :], jnp.sin(angles)[:, None, :])


def rotate(values, cosine_table, sine_table):
    half_width = values.shape[-1] // 2
    lead_half = values[..., :half_width]
    tail_half = values[..., half_width:]
    return jnp.concatenate(
        [
            lead_half * cosine_table - tail_half * sine_table,
            tail_half * cosine_table + lead_half * sine_table,
        ],
        axis=-1,
    )


def attention_scores(queries, key_rows, segments):
    length, heads_here, head_width = queries.shape
    kv_here = key_rows.shape[1]
    grouped = queries.reshape(length, kv_here, heads_here // kv_here, head_width)
    scores = (
        jnp.einsum("qkgd,tkd->kgqt", grouped, key_rows, preferred_element_type=jnp.float32)
        * attn_scale
    )
    places = jnp.arange(length)
    allowed = (places[:, None] >= places[None, :]) & (segments[:, None] == segments[None, :])
    return (jnp.where(allowed, scores, masked_value), grouped)


def attend_forward(pieces):
    queries, key_rows, value_rows, segments = pieces
    scores, grouped = attention_scores(queries, key_rows, segments)
    row_top = jnp.max(scores, axis=-1, keepdims=True)
    raised = jnp.exp(scores - row_top)
    row_total = jnp.sum(raised, axis=-1, keepdims=True)
    probs_low = (raised / row_total).astype(jnp.bfloat16)
    mixed_out = jnp.einsum(
        "kgqt,tkd->qkgd", probs_low, value_rows, preferred_element_type=jnp.float32
    )
    return (
        mixed_out.astype(jnp.bfloat16).reshape(queries.shape[0], -1),
        (row_top + jnp.log(row_total))[..., 0],
    )


def attend_backward(pieces):
    queries, key_rows, value_rows, segments, logsum, mixed_grad = pieces
    scores, grouped = attention_scores(queries, key_rows, segments)
    attn_probs = jnp.exp(scores - logsum[..., None])
    grad_grouped = mixed_grad.reshape(grouped.shape)
    probs_grad = jnp.einsum(
        "qkgd,tkd->kgqt", grad_grouped, value_rows, preferred_element_type=jnp.float32
    )
    row_inner = jnp.sum(attn_probs * probs_grad, axis=-1, keepdims=True)
    score_grad = (attn_probs * (probs_grad - row_inner)).astype(jnp.bfloat16)
    query_grad = (
        jnp.einsum("kgqt,tkd->qkgd", score_grad, key_rows, preferred_element_type=jnp.float32)
        * attn_scale
    )
    key_grad = (
        jnp.einsum("kgqt,qkgd->tkd", score_grad, grouped, preferred_element_type=jnp.float32)
        * attn_scale
    )
    value_grad = jnp.einsum(
        "kgqt,qkgd->tkd",
        attn_probs.astype(jnp.bfloat16),
        grad_grouped,
        preferred_element_type=jnp.float32,
    )
    return (query_grad.reshape(queries.shape), key_grad, value_grad)


def route_slots(expert, group_routes, group_gates, capacity):
    hit_mask = group_routes == expert
    member = jnp.any(hit_mask, axis=1)
    weight = jnp.sum(jnp.where(hit_mask, group_gates.astype(jnp.float32), 0.0), axis=1)
    member_int = member.astype(jnp.int32)
    slot_index = jnp.cumsum(member_int) - 1
    target = jnp.where(member, slot_index, capacity)
    row_ids = jnp.arange(member.shape[0], dtype=jnp.int32)
    slot_rows = jnp.zeros((capacity,), jnp.int32).at[target].set(row_ids, mode="drop")
    filled = jnp.arange(capacity) < jnp.sum(member_int)
    slot_scale = jnp.where(filled, jnp.take(weight, slot_rows, axis=0), 0.0)
    picked = jnp.where(filled[:, None], jnp.take(hit_mask, slot_rows, axis=0), False).astype(
        jnp.float32
    )
    return (slot_rows, slot_scale, picked)


def local(
    emb,
    segment_ids,
    routes,
    norm1_gain,
    w_query,
    w_key,
    w_value,
    w_out,
    norm2_gain,
    w_router,
    w_gate,
    w_up,
    w_down,
    cotangent,
):
    local_rows = emb.shape[0]
    query_w, key_w, value_w, out_w, router_w, gate_w, up_w, down_w = (
        lax.all_gather(w_query, "fsdp", axis=0, tiled=True),
        lax.all_gather(w_key, "fsdp", axis=0, tiled=True),
        lax.all_gather(w_value, "fsdp", axis=0, tiled=True),
        lax.all_gather(w_out, "fsdp", axis=0, tiled=True),
        lax.all_gather(w_router, "fsdp", axis=0, tiled=True),
        lax.all_gather(w_gate, "fsdp", axis=1, tiled=True),
        lax.all_gather(w_up, "fsdp", axis=1, tiled=True),
        lax.all_gather(w_down, "fsdp", axis=1, tiled=True),
    )
    gain_one = norm1_gain.astype(jnp.float32)
    gain_two = norm2_gain.astype(jnp.float32)
    start_x = emb.astype(jnp.float32) * emb_scale
    normed_one, inverse_one = rms_forward(start_x, gain_one)
    group_rows = lax.all_gather(normed_one.astype(jnp.bfloat16), "tp", axis=0, tiled=True)
    group_size = group_rows.shape[0]
    seq_count = group_size // SEQ
    heads_here = query_w.shape[1] // HEAD_DIM
    kv_here = key_w.shape[1] // HEAD_DIM
    cosine_table, sine_table = rotary_tables(group_size, HEAD_DIM)
    query_proj = jnp.dot(group_rows, query_w, preferred_element_type=jnp.float32).reshape(
        group_size, heads_here, HEAD_DIM
    )
    key_proj = jnp.dot(group_rows, key_w, preferred_element_type=jnp.float32).reshape(
        group_size, kv_here, HEAD_DIM
    )
    queries = rotate(query_proj, cosine_table, sine_table).astype(jnp.bfloat16)
    key_rows = rotate(key_proj, cosine_table, sine_table).astype(jnp.bfloat16)
    value_rows = jnp.dot(group_rows, value_w, preferred_element_type=jnp.float32).astype(
        jnp.bfloat16
    )
    seq_queries = queries.reshape(seq_count, SEQ, heads_here, HEAD_DIM)
    seq_keys = key_rows.reshape(seq_count, SEQ, kv_here, HEAD_DIM)
    seq_values = value_rows.reshape(seq_count, SEQ, kv_here, HEAD_DIM)
    mixed_out, logsum = lax.map(attend_forward, (seq_queries, seq_keys, seq_values, segment_ids))
    mixed_rows = mixed_out.reshape(group_size, heads_here * HEAD_DIM)
    attn_branch = lax.psum_scatter(
        contract_last(mixed_rows, out_w), "tp", scatter_dimension=0, tiled=True
    )
    mid_x = start_x + resid_scale * attn_branch
    normed_two, inverse_two = rms_forward(mid_x, gain_two)
    normed_low = normed_two.astype(jnp.bfloat16)
    logits = jnp.dot(normed_low, router_w, preferred_element_type=jnp.float32)
    tp_index = lax.axis_index("tp")
    own_routes = lax.dynamic_slice_in_dim(routes, tp_index * local_rows, local_rows, 0)
    expert_count = router_w.shape[1]
    chosen = (own_routes[:, :, None] == jnp.arange(expert_count)[None, None, :]).astype(jnp.float32)
    selected = jnp.sum(chosen * logits[:, None, :], axis=-1)
    sel_top = jnp.max(selected, axis=-1, keepdims=True)
    sel_raised = jnp.exp(selected - sel_top)
    gates = sel_raised / jnp.sum(sel_raised, axis=-1, keepdims=True)
    moe_rows, group_gates = (
        lax.all_gather(normed_low, "tp", axis=0, tiled=True),
        lax.all_gather(gates.astype(jnp.bfloat16), "tp", axis=0, tiled=True),
    )
    experts_here = gate_w.shape[0]
    capacity = group_size * routes.shape[1] // expert_count * 2
    expert_ids = tp_index * experts_here + jnp.arange(experts_here, dtype=jnp.int32)

    def expert_forward(running, inputs):
        gate_one, up_one, down_one, expert = inputs
        slot_rows, slot_scale, picked = route_slots(expert, routes, group_gates, capacity)
        rows_taken = jnp.take(moe_rows, slot_rows, axis=0)
        gate_pre = jnp.dot(rows_taken, gate_one, preferred_element_type=jnp.float32)
        up_pre = jnp.dot(rows_taken, up_one, preferred_element_type=jnp.float32)
        act_low = (gate_pre * jax.nn.sigmoid(gate_pre) * up_pre).astype(jnp.bfloat16)
        expert_out = contract_last(act_low, down_one)
        running = running.at[slot_rows].add(expert_out * slot_scale[:, None])
        return (running, (slot_rows, slot_scale, picked, gate_pre, up_pre, act_low, expert_out))

    moe_start = jnp.zeros((group_size, moe_rows.shape[1]), jnp.float32)
    moe_part, kept = lax.scan(expert_forward, moe_start, (gate_w, up_w, down_w, expert_ids))
    moe_sum = lax.psum_scatter(moe_part, "tp", scatter_dimension=0, tiled=True)
    out = (mid_x + resid_scale * moe_sum).astype(jnp.bfloat16)
    out_grad = cotangent.astype(jnp.float32)
    moe_grad = (resid_scale * out_grad).astype(jnp.bfloat16)
    moe_grad_rows = lax.all_gather(moe_grad, "tp", axis=0, tiled=True)
    gate_back, up_back, down_back = (gate_w, up_w, down_w)

    def expert_backward(running, inputs):
        rows_grad, gates_part = running
        (
            gate_one,
            up_one,
            down_one,
            slot_rows,
            slot_scale,
            picked,
            gate_pre,
            up_pre,
            act_low,
            expert_out,
        ) = inputs
        rows_taken = jnp.take(moe_rows, slot_rows, axis=0)
        taken_grad = jnp.take(moe_grad_rows, slot_rows, axis=0).astype(jnp.float32)
        slot_grad = jnp.sum(expert_out * taken_grad, axis=1)
        gates_part = gates_part.at[slot_rows].add(picked * slot_grad[:, None])
        scaled_grad = (taken_grad * slot_scale[:, None]).astype(jnp.bfloat16)
        down_grad = contract_first(scaled_grad, act_low)
        act_grad = jnp.dot(scaled_grad, down_one, preferred_element_type=jnp.float32)
        sig_gate = jax.nn.sigmoid(gate_pre)
        gate_grad = (act_grad * up_pre * sig_gate * (1.0 + gate_pre * (1.0 - sig_gate))).astype(
            jnp.bfloat16
        )
        up_grad = (act_grad * gate_pre * sig_gate).astype(jnp.bfloat16)
        gate_w_grad = contract_first(rows_taken, gate_grad)
        up_w_grad = contract_first(rows_taken, up_grad)
        input_grad = contract_last(gate_grad, gate_one) + contract_last(up_grad, up_one)
        rows_grad = rows_grad.at[slot_rows].add(input_grad)
        return ((rows_grad, gates_part), (gate_w_grad, up_w_grad, down_grad))

    back_start = (
        jnp.zeros((group_size, moe_rows.shape[1]), jnp.float32),
        jnp.zeros((group_size, routes.shape[1]), jnp.float32),
    )
    (rows_grad_part, gates_grad_part), (gate_grads, up_grads, down_grads) = lax.scan(
        expert_backward, back_start, (gate_back, up_back, down_back) + kept
    )
    rows_grad_sum, gates_grad = (
        lax.psum_scatter(rows_grad_part, "tp", scatter_dimension=0, tiled=True),
        lax.psum_scatter(gates_grad_part, "tp", scatter_dimension=0, tiled=True),
    )
    gates_inner = jnp.sum(gates * gates_grad, axis=-1, keepdims=True)
    selected_grad = gates * (gates_grad - gates_inner)
    logits_grad = jnp.sum(chosen * selected_grad[:, :, None], axis=1).astype(jnp.bfloat16)
    router_grad_part = contract_first(normed_low, logits_grad)
    normed_two_grad = rows_grad_sum + contract_last(logits_grad, router_w)
    mid_from_norm, gain_two_grad = rms_backward(normed_two_grad, mid_x, inverse_two, gain_two)
    mid_grad = out_grad + mid_from_norm
    branch_grad = (resid_scale * mid_grad).astype(jnp.bfloat16)
    branch_grad_rows = lax.all_gather(branch_grad, "tp", axis=0, tiled=True)
    out_w_grad = contract_first(branch_grad_rows, mixed_rows)
    mixed_grad = jnp.dot(branch_grad_rows, out_w, preferred_element_type=jnp.float32).astype(
        jnp.bfloat16
    )
    query_grad, key_grad, value_grad = lax.map(
        attend_backward,
        (
            seq_queries,
            seq_keys,
            seq_values,
            segment_ids,
            logsum,
            mixed_grad.reshape(seq_count, SEQ, -1),
        ),
    )
    query_proj_grad = (
        rotate(query_grad.reshape(group_size, heads_here, HEAD_DIM), cosine_table, -sine_table)
        .astype(jnp.bfloat16)
        .reshape(group_size, -1)
    )
    key_proj_grad = (
        rotate(key_grad.reshape(group_size, kv_here, HEAD_DIM), cosine_table, -sine_table)
        .astype(jnp.bfloat16)
        .reshape(group_size, -1)
    )
    value_proj_grad = value_grad.reshape(group_size, -1).astype(jnp.bfloat16)
    query_w_grad = contract_first(group_rows, query_proj_grad)
    key_w_grad = contract_first(group_rows, key_proj_grad)
    value_w_grad = contract_first(group_rows, value_proj_grad)
    total_grad = contract_last(query_proj_grad, query_w)
    total_grad = total_grad + contract_last(key_proj_grad, key_w)
    normed_one_grad = lax.psum_scatter(
        total_grad + contract_last(value_proj_grad, value_w), "tp", scatter_dimension=0, tiled=True
    )
    start_from_norm, gain_one_grad = rms_backward(normed_one_grad, start_x, inverse_one, gain_one)
    grad_emb = emb_scale * (mid_grad + start_from_norm)
    gain_one_sum, gain_two_sum, router_sum = lax.psum(
        (gain_one_grad, gain_two_grad, router_grad_part), ("fsdp", "tp")
    )
    router_rows = w_router.shape[0]
    router_own = lax.dynamic_slice_in_dim(
        router_sum, lax.axis_index("fsdp") * router_rows, router_rows, 0
    )
    query_sum, key_sum, value_sum, out_sum = (
        lax.psum_scatter(query_w_grad, "fsdp", scatter_dimension=0, tiled=True),
        lax.psum_scatter(key_w_grad, "fsdp", scatter_dimension=0, tiled=True),
        lax.psum_scatter(value_w_grad, "fsdp", scatter_dimension=0, tiled=True),
        lax.psum_scatter(out_w_grad, "fsdp", scatter_dimension=0, tiled=True),
    )
    gate_sum, up_sum, down_sum = (
        lax.psum_scatter(gate_grads, "fsdp", scatter_dimension=1, tiled=True),
        lax.psum_scatter(up_grads, "fsdp", scatter_dimension=1, tiled=True),
        lax.psum_scatter(down_grads, "fsdp", scatter_dimension=1, tiled=True),
    )
    return (
        out,
        grad_emb,
        gain_one_sum,
        query_sum,
        key_sum,
        value_sum,
        out_sum,
        gain_two_sum,
        router_own,
        gate_sum,
        up_sum,
        down_sum,
    )


def solution(mesh):
    return jax.shard_map(
        local,
        mesh=mesh,
        in_specs=(
            P(("fsdp", "tp"), None),
            P("fsdp", None),
            P("fsdp", None),
            P(),
            P("fsdp", "tp"),
            P("fsdp", "tp"),
            P("fsdp", "tp"),
            P("fsdp", "tp"),
            P(),
            P("fsdp", None),
            P("tp", "fsdp", None),
            P("tp", "fsdp", None),
            P("tp", "fsdp", None),
            P(("fsdp", "tp"), None),
        ),
        out_specs=(
            P(("fsdp", "tp"), None),
            P(("fsdp", "tp"), None),
            P(),
            P("fsdp", "tp"),
            P("fsdp", "tp"),
            P("fsdp", "tp"),
            P("fsdp", "tp"),
            P(),
            P("fsdp", None),
            P("tp", "fsdp", None),
            P("tp", "fsdp", None),
            P("tp", "fsdp", None),
        ),
        check_vma=False,
    )
```

profile of v0, /device:TPU:0, one launch (start us, length us, event | category | flops | bytes accessed | tf_op | source)
XLA Modules:
  0.0 2862.0 jit_solution(5613374487226321994)
XLA Ops:
  37.2 41.9 %all-gather.11.cloned.1.call-done = bf16[1024,1536]{1,0:T(8,128)(2,1)} async-done(((bf16[256,1536]{1,0:T(8,128)(2,1)}), bf16[1024,1536]{1,0:T(8,128)(2,1)}) %all-gather.11.cloned.1.call-update) | async-done | bytes 3145744 | tf_op jit(solution)/shard_map/all_gather | solution.py:166
  136.1 110.3 %reduce-scatter.13.cloned.1.call-done = f32[256,1536]{1,0:T(8,128)} async-done(((f32[1024,1536]{1,0:T(8,128)}), f32[256,1536]{1,0:T(8,128)}) %reduce-scatter.13.cloned.1.call-update) | async-done | bytes 1572880 | tf_op jit(solution)/shard_map/reduce_scatter | solution.py:188
  280.6 34.2 %all-gather.17.cloned.1.call-done = bf16[1024,1536]{1,0:T(8,128)(2,1)} async-done(((bf16[256,1536]{1,0:T(8,128)(2,1)}), bf16[1024,1536]{1,0:T(8,128)(2,1)}) %all-gather.17.cloned.1.call-update) | async-done | bytes 3145744 | tf_op jit(solution)/shard_map/all_gather | solution.py:204
  314.8 85.7 %all-gather.19.cloned.1.call-done = bf16[10,1536,512]{2,1,0:T(8,128)(2,1)} async-done(((bf16[10,192,512]{2,1,0:T(8,128)(2,1)}), bf16[10,1536,512]{2,1,0:T(8,128)(2,1)}) %all-gather.19.cloned.1.call-update) | async-done | bytes 15728656 | tf_op jit(solution)/shard_map/all_gather | solution.py:158
  400.5 87.2 %all-gather.21.cloned.1.call-done = bf16[10,1536,512]{2,1,0:T(8,128)(2,1)} async-done(((bf16[10,192,512]{2,1,0:T(8,128)(2,1)}), bf16[10,1536,512]{2,1,0:T(8,128)(2,1)}) %all-gather.21.cloned.1.call-update) | async-done | bytes 15728656 | tf_op jit(solution)/shard_map/all_gather | solution.py:159
  487.8 87.2 %all-gather.23.cloned.1.call-done = bf16[10,1536,512]{2,1,0:T(8,128)(2,1)} async-done(((bf16[10,192,512]{2,1,0:T(8,128)(2,1)}), bf16[10,1536,512]{2,1,0:T(8,128)(2,1)}) %all-gather.23.cloned.1.call-update) | async-done | bytes 15728656 | tf_op jit(solution)/shard_map/all_gather | solution.py:160
  578.4 468.3 %while.71 = (s32[]{:T(128)}, f32[1024,1536]{1,0:T(8,128)}, s32[10,408]{1,0:T(8,128)}, f32[10,408]{1,0:T(8,128)}, f32[10,408,8]{2,1,0:T(8,128)}, /*index=5*/f32[1...) while((s32[]{:T(128)}, f32[1024,1536]{1,0:T(8,128)}, ...), condition=%wide.region_18.20_spmd, body=%wide.region_10.19_spmd.sunk | while | flops 1929139968 | bytes 35207396 | solution.py:223
  1050.9 505.1 %while.72 = (s32[]{:T(128)}, f32[1024,1536]{1,0:T(8,128)}, f32[1024,8]{1,0:T(8,128)}, f32[10,1536,512]{2,1,0:T(8,128)}, f32[10,1536,512]{2,1,0:T(8,128)}, /*inde...) while((s32[]{:T(128)}, f32[1024,1536]{1,0:T(8,128)}, ...), condition=%wide.region_24.26_spmd, body=%wide.region_20.25_spmd.sunk | while | flops 3863125760 | bytes 57883772 | solution.py:267
  1558.7 18.9 reduce-scatter.19.cloned.1.call-done
  1579.1 109.7 %reduce-scatter.17.cloned.1.call-done = f32[256,1536]{1,0:T(8,128)} async-done(((f32[1024,1536]{1,0:T(8,128)}), f32[256,1536]{1,0:T(8,128)}) %reduce-scatter.17.cloned.1.call-update) | async-done | bytes 1572880 | tf_op jit(solution)/shard_map/reduce_scatter | solution.py:271
  1694.7 63.0 %all-gather.27.cloned.1.call-done = bf16[1024,1536]{1,0:T(8,128)(2,1)} async-done(((bf16[256,1536]{1,0:T(8,128)(2,1)}), bf16[1024,1536]{1,0:T(8,128)(2,1)}) %all-gather.27.cloned.1.call-update) | async-done | bytes 3145744 | tf_op jit(solution)/shard_map/all_gather | solution.py:282
  1762.5 65.1 %while.73 = (s32[]{:T(128)}, f32[2,512,6,64]{1,0,3,2:T(2,128)}, f32[2,512,2,64]{1,0,3,2:T(2,128)}, bf16[2,512,2,64]{1,3,2,0:T(8,128)(2,1)}, bf16[2,512,2,64]{1,3...) while((s32[]{:T(128)}, f32[2,512,6,64]{1,0,3,2:T(2,128)}, ...), condition=%wide.region_32.34_spmd, body=%wide.region_30.33_spmd.sunk | while | flops 1031271424 | bytes 58161316 | solution.py:287
  1780.1 15.0 dynamic_update_slice.116
  1860.1 27.0 all-reduce.3.cloned.1.call-done
  1888.6 111.7 %reduce-scatter.21.cloned.1.call-done = f32[256,1536]{1,0:T(8,128)} async-done(((f32[1024,1536]{1,0:T(8,128)}), f32[256,1536]{1,0:T(8,128)}) %reduce-scatter.21.cloned.1.call-update) | async-done | bytes 1572880 | tf_op jit(solution)/shard_map/reduce_scatter | solution.py:314
  2002.3 45.1 %all-reduce = (f32[1536]{0:T(1024)}, f32[1536]{0:T(1024)}) all-reduce(f32[1536]{0:T(1024)S(1)} %get-tuple-element.575, f32[1536]{0:T(1024)S(1)} %get-tuple-element.573), channel_id=1, replica_groups=mesh['fsdp'=8,'tp'=4] {'fsdp','tp'}, use_global_device_ids=true, to_apply=%region_36.38 | all-reduce | flops 3072 | bytes 24576 | tf_op jit(solution)/shard_map/psum | solution.py:319
  2047.3 67.5 %reduce-scatter.15.cloned.1.call-done = f32[256,1536]{1,0:T(8,128)} async-done(((f32[1024,1536]{1,0:T(8,128)}), f32[256,1536]{1,0:T(8,128)}) %reduce-scatter.15.cloned.1.call-update) | async-done | bytes 1572880 | tf_op jit(solution)/shard_map/reduce_scatter | solution.py:224
  2119.5 34.4 %reduce-scatter.25.cloned.1.call-done = f32[192,128]{1,0:T(8,128)} async-done(((f32[1536,128]{1,0:T(8,128)}), f32[192,128]{1,0:T(8,128)}) %reduce-scatter.25.cloned.1.call-update) | async-done | bytes 98320 | tf_op jit(solution)/shard_map/reduce_scatter | solution.py:328
  2153.9 38.6 %reduce-scatter.27.cloned.1.call-done = f32[192,128]{1,0:T(8,128)} async-done(((f32[1536,128]{1,0:T(8,128)}), f32[192,128]{1,0:T(8,128)}) %reduce-scatter.27.cloned.1.call-update) | async-done | bytes 98320 | tf_op jit(solution)/shard_map/reduce_scatter | solution.py:329
  2192.5 46.2 %reduce-scatter.29.cloned.1.call-done = f32[192,384]{1,0:T(8,128)} async-done(((f32[1536,384]{1,0:T(8,128)}), f32[192,384]{1,0:T(8,128)}) %reduce-scatter.29.cloned.1.call-update) | async-done | bytes 294928 | tf_op jit(solution)/shard_map/reduce_scatter | solution.py:330
  2238.7 46.3 %reduce-scatter.23.cloned.1.call-done = f32[192,384]{1,0:T(8,128)} async-done(((f32[1536,384]{1,0:T(8,128)}), f32[192,384]{1,0:T(8,128)}) %reduce-scatter.23.cloned.1.call-update) | async-done | bytes 294928 | tf_op jit(solution)/shard_map/reduce_scatter | solution.py:327
  2284.9 189.9 %reduce-scatter.35.cloned.1.call-done = f32[10,192,512]{2,1,0:T(8,128)} async-done(((f32[10,1536,512]{2,1,0:T(8,128)}), f32[10,192,512]{2,1,0:T(8,128)}) %reduce-scatter.35.cloned.1.call-update) | async-done | bytes 3932176 | tf_op jit(solution)/shard_map/reduce_scatter | solution.py:335
  2474.8 190.1 %reduce-scatter.31.cloned.1.call-done = f32[10,192,512]{2,1,0:T(8,128)} async-done(((f32[10,1536,512]{2,1,0:T(8,128)}), f32[10,192,512]{2,1,0:T(8,128)}) %reduce-scatter.31.cloned.1.call-update) | async-done | bytes 3932176 | tf_op jit(solution)/shard_map/reduce_scatter | solution.py:333
  2664.9 190.0 %reduce-scatter.33.cloned.1.call-done = f32[10,192,512]{2,1,0:T(8,128)} async-done(((f32[10,1536,512]{2,1,0:T(8,128)}), f32[10,192,512]{2,1,0:T(8,128)}) %reduce-scatter.33.cloned.1.call-update) | async-done | bytes 3932176 | tf_op jit(solution)/shard_map/reduce_scatter | solution.py:334
  (952 shorter events, 1217.8 us)
Async XLA Ops:
  7.2 71.9 %all-gather.11.cloned.1.call-start = ((), (), s32[]{:S(2)}) async-start(), calls=%async_computation.12 | async-start | bytes 3932160 | tf_op jit(solution)/shard_map/all_gather | solution.py:166
  12.8 90.8 %all-gather.13.cloned.1.call-start = ((), (), s32[]{:S(2)}) async-start(), calls=%async_computation.13 | async-start | bytes 1327104 | tf_op jit(solution)/shard_map/all_gather | solution.py:153
  13.5 115.9 %all-gather.15.cloned.1.call-start = ((), (), s32[]{:S(2)}) async-start(), calls=%async_computation.14 | async-start | bytes 1327104 | tf_op jit(solution)/shard_map/all_gather | solution.py:156
  14.3 232.1 %reduce-scatter.13.cloned.1.call-start = ((), (), s32[]{:S(2)}) async-start(), calls=%async_computation.15 | async-start | bytes 7864320 | tf_op jit(solution)/shard_map/reduce_scatter | solution.py:188
  135.5 179.3 %all-gather.17.cloned.1.call-start = ((), (), s32[]{:S(2)}) async-start(), calls=%async_computation.16 | async-start | bytes 3932160 | tf_op jit(solution)/shard_map/all_gather | solution.py:204
  250.5 150.0 %all-gather.19.cloned.1.call-start = ((), (), s32[]{:S(2)}) async-start(), calls=%async_computation.17 | async-start | bytes 17694720 | tf_op jit(solution)/shard_map/all_gather | solution.py:158
  251.1 236.7 %all-gather.21.cloned.1.call-start = ((), (), s32[]{:S(2)}) async-start(), calls=%async_computation.18 | async-start | bytes 17694720 | tf_op jit(solution)/shard_map/all_gather | solution.py:159
  251.9 323.1 %all-gather.23.cloned.1.call-start = ((), (), s32[]{:S(2)}) async-start(), calls=%async_computation.19 | async-start | bytes 17694720 | tf_op jit(solution)/shard_map/all_gather | solution.py:160
  252.6 794.1 %all-gather.25.cloned.1.call-start = ((), (), s32[]{:S(2)}) async-start(), calls=%async_computation.21 | async-start | bytes 3932160 | tf_op jit(solution)/shard_map/all_gather | solution.py:228
  253.7 1323.9 %reduce-scatter.19.cloned.1.call-start = ((), (), s32[]{:S(2)}) async-start(), calls=%async_computation.23 | async-start | bytes 40960 | tf_op jit(solution)/shard_map/reduce_scatter | solution.py:272
  314.8 263.6 %copy-start = (bf16[1024,1536]{1,0:T(8,128)(2,1)S(1)}, bf16[1024,1536]{1,0:T(8,128)(2,1)}, u32[]{:S(2)}) copy-start(bf16[1024,1536]{1,0:T(8,128)(2,1)} %all-gather.17.cloned.1.call-done) | copy-start | bytes 9437188
  1557.9 130.9 %reduce-scatter.17.cloned.1.call-start = ((), (), s32[]{:S(2)}) async-start(), calls=%async_computation.22 | async-start | bytes 7864320 | tf_op jit(solution)/shard_map/reduce_scatter | solution.py:271
  1558.6 199.0 %all-gather.27.cloned.1.call-start = ((), (), s32[]{:S(2)}) async-start(), calls=%async_computation.24 | async-start | bytes 3932160 | tf_op jit(solution)/shard_map/all_gather | solution.py:282
  1693.5 193.6 %all-reduce.3.cloned.1.call-start = ((), (), s32[]{:S(2)}) async-start(), calls=%async_computation.30 | async-start | bytes 491520 | tf_op jit(solution)/shard_map/psum | solution.py:319
  1694.6 305.7 %reduce-scatter.21.cloned.1.call-start = ((), (), s32[]{:S(2)}) async-start(), calls=%async_computation.25 | async-start | bytes 7864320 | tf_op jit(solution)/shard_map/reduce_scatter | solution.py:314
  1841.3 273.5 %reduce-scatter.15.cloned.1.call-start = ((), (), s32[]{:S(2)}) async-start(), calls=%async_computation.20 | async-start | bytes 7864320 | tf_op jit(solution)/shard_map/reduce_scatter | solution.py:224
  1841.9 312.0 %reduce-scatter.25.cloned.1.call-start = ((), (), s32[]{:S(2)}) async-start(), calls=%async_computation.27 | async-start | bytes 884736 | tf_op jit(solution)/shard_map/reduce_scatter | solution.py:328
  1845.2 347.3 %reduce-scatter.27.cloned.1.call-start = ((), (), s32[]{:S(2)}) async-start(), calls=%async_computation.28 | async-start | bytes 884736 | tf_op jit(solution)/shard_map/reduce_scatter | solution.py:329
  1848.1 390.6 %reduce-scatter.29.cloned.1.call-start = ((), (), s32[]{:S(2)}) async-start(), calls=%async_computation.29 | async-start | bytes 2654208 | tf_op jit(solution)/shard_map/reduce_scatter | solution.py:330
  1853.5 431.5 %reduce-scatter.23.cloned.1.call-start = ((), (), s32[]{:S(2)}) async-start(), calls=%async_computation.26 | async-start | bytes 2654208 | tf_op jit(solution)/shard_map/reduce_scatter | solution.py:327
  1858.0 616.9 %reduce-scatter.35.cloned.1.call-start = ((), (), s32[]{:S(2)}) async-start(), calls=%async_computation.33 | async-start | bytes 35389440 | tf_op jit(solution)/shard_map/reduce_scatter | solution.py:335
  1858.6 806.3 %reduce-scatter.31.cloned.1.call-start = ((), (), s32[]{:S(2)}) async-start(), calls=%async_computation.31 | async-start | bytes 35389440 | tf_op jit(solution)/shard_map/reduce_scatter | solution.py:333
  1859.3 995.6 %reduce-scatter.33.cloned.1.call-start = ((), (), s32[]{:S(2)}) async-start(), calls=%async_computation.32 | async-start | bytes 35389440 | tf_op jit(solution)/shard_map/reduce_scatter | solution.py:334
  1859.4 255.5 %copy-start.67 = (f32[256]{0:T(256)S(1)}, f32[256]{0:T(256)}, u32[]{:S(2)}) copy-start(f32[256]{0:T(256)} %get-tuple-element.715) | copy-start | bytes 3076
  (161 other events, 2877.8 us)
Sparse Core Ops, SparseCore 0:
  12.9 66.1 all-gather.10
  81.0 22.5 all-gather.12
  105.5 23.9 all-gather.14
  135.6 110.7 reduce-scatter.12
  250.6 64.1 all-gather.16
  316.5 83.9 all-gather.18
  402.4 85.2 all-gather.20
  489.6 85.2 all-gather.22
  577.1 63.4 all-gather.24
  1558.0 19.4 reduce-scatter.18
  1579.9 108.8 reduce-scatter.16
  1693.6 63.9 all-gather.26
  1763.1 123.8 all-reduce.2
  1889.2 111.0 reduce-scatter.20
  2002.5 112.3 reduce-scatter.14
  2118.4 35.4 reduce-scatter.24
  2157.5 34.9 reduce-scatter.26
  2196.2 42.3 reduce-scatter.28
  2242.6 42.3 reduce-scatter.22
  2289.0 185.8 reduce-scatter.34
  2479.0 185.8 reduce-scatter.30
  2669.1 185.7 reduce-scatter.32
where the time goes:
time: 2880 us; the launch traced here: 2860 us
  waiting for transfers between devices  1610 us (56%)
  other arithmetic  412 us (14%)
  matrix products  385 us (13%)
  local copies, waits for them, and re-layouts  348 us (12%)
  blocking collectives  90.3 us (3%)
    reduce_scatter x1, waiting for transfers between devices, local(): lax.psum_scatter(gate_grads, 'fsdp', scatter_dimension=1, tiled=True)  190 us
    reduce_scatter x1, waiting for transfers between devices, local(): lax.psum_scatter(up_grads, 'fsdp', scatter_dimension=1, tiled=True)  190 us
    reduce_scatter x1, waiting for transfers between devices, local(): lax.psum_scatter(down_grads, 'fsdp', scatter_dimension=1, tiled=True)  190 us
    dot_general x35, matrix products, contract_last(): lax.dot_general(left_op, right_op, (((1,), (1,)), ((), ())), preferred_el...  122 us
    dot_general x35, matrix products, contract_first(): lax.dot_general(left_op, right_op, (((0,), (0,)), ((), ())), preferred_el...  117 us
    scatter-add x10, other arithmetic, expert_forward(): running = running.at[slot_rows].add(expert_out * slot_scale[:, None])  112 us
    reduce_scatter x1, waiting for transfers between devices, local(): lax.psum_scatter(total_grad + contract_last(value_proj_grad, value_w), 't...  112 us
    reduce_scatter x1, waiting for transfers between devices, local(): lax.psum_scatter(contract_last(mixed_rows, out_w), 'tp', scatter_dimensio...  110 us
  transfers between devices with their start and end apart: 22, of which 21 were waited for; matrix products, arithmetic and copies ran while one was open for 21% of the time, Pallas kernels for 0%

commit v1 on v0

--- a/solution.py
+++ b/solution.py
@@ -11,6 +11,27 @@
 norm_eps = 1e-06
 rope_base = 10000.0
 masked_value = -1e30
+
+
+def joined_along(pieces, dim):
+    lengths = list(pieces.shape[1:])
+    lengths[dim] *= pieces.shape[0]
+    return jnp.moveaxis(pieces, 0, dim).reshape(lengths)
+
+
+def grow_blocks(value, axis):
+    size, place = (lax.axis_size(axis), lax.axis_index(axis))
+    tiles, bit = (value[None], 1)
+    while bit < size:
+        other = lax.ppermute(tiles, axis, [(i, i ^ bit) for i in range(size)])
+        low = place & bit == 0
+        tiles = jnp.concatenate([jnp.where(low, tiles, other), jnp.where(low, other, tiles)])
+        bit *= 2
+    return tiles
+
+
+def gather_by_bits(x, axis, dim):
+    return joined_along(grow_blocks(x, axis), dim)
 
 
 def contract_last(left_op, right_op):
@@ -156,7 +177,7 @@
         lax.all_gather(w_out, "fsdp", axis=0, tiled=True),
         lax.all_gather(w_router, "fsdp", axis=0, tiled=True),
         lax.all_gather(w_gate, "fsdp", axis=1, tiled=True),
-        lax.all_gather(w_up, "fsdp", axis=1, tiled=True),
+        gather_by_bits(w_up, "fsdp", 1),
         lax.all_gather(w_down, "fsdp", axis=1, tiled=True),
     )
     gain_one = norm1_gain.astype(jnp.float32)

time: 2880 us -> 2980 us (1.035)
  blocking collectives: 90.3 us -> 348 us
  waiting for transfers between devices: 1610 us -> 1420 us
    all_gather x1, blocking collectives: 9.38 us -> 268 us  [local(): lax.all_gather(w_router, 'fsdp', axis=0, tiled=True)]
    ppermute x0 -> x3, waiting for transfers between devices: none -> 111 us  [grow_blocks(): other = lax.ppermute(tiles, axis, [(i, i ^ bit) for i in range(size)])]
    all_gather x1 -> x0, waiting for transfers between devices: 87.2 us -> none  [local(): lax.all_gather(w_up, 'fsdp', axis=1, tiled=True)]
    all_gather x1, waiting for transfers between devices: 87.2 us -> 0.02 us  [local(): lax.all_gather(w_down, 'fsdp', axis=1, tiled=True)]
    all_gather x1, waiting for transfers between devices: 85.7 us -> 0.02 us  [local(): lax.all_gather(w_gate, 'fsdp', axis=1, tiled=True)]
    all_gather x1, waiting for transfers between devices: 34.2 us -> 0.02 us  [local(): lax.all_gather(normed_low, 'tp', axis=0, tiled=True)]
  transfers between devices with their start and end apart: 22 -> 24, of which waited for: 21 -> 19; matrix products, arithmetic and copies ran while one was open for 21% -> 22% of each run, Pallas kernels for 0% -> 0%
where the time goes in v1:
time: 2980 us; the launch traced here: 2970 us
  waiting for transfers between devices  1420 us (48%)
  other arithmetic  437 us (15%)
  matrix products  385 us (13%)
  local copies, waits for them, and re-layouts  354 us (12%)
  blocking collectives  348 us (12%)
    all_gather x1, blocking collectives, local(): lax.all_gather(w_router, 'fsdp', axis=0, tiled=True)  268 us
    reduce_scatter x1, waiting for transfers between devices, local(): lax.psum_scatter(down_grads, 'fsdp', scatter_dimension=1, tiled=True)  190 us
    reduce_scatter x1, waiting for transfers between devices, local(): lax.psum_scatter(up_grads, 'fsdp', scatter_dimension=1, tiled=True)  190 us
    reduce_scatter x1, waiting for transfers between devices, local(): lax.psum_scatter(gate_grads, 'fsdp', scatter_dimension=1, tiled=True)  190 us
    dot_general x35, matrix products, contract_last(): lax.dot_general(left_op, right_op, (((1,), (1,)), ((), ())), preferred_el...  122 us
    dot_general x35, matrix products, contract_first(): lax.dot_general(left_op, right_op, (((0,), (0,)), ((), ())), preferred_el...  117 us
    scatter-add x10, other arithmetic, expert_forward(): running = running.at[slot_rows].add(expert_out * slot_scale[:, None])  112 us
    reduce_scatter x1, waiting for transfers between devices, local(): lax.psum_scatter(total_grad + contract_last(value_proj_grad, value_w), 't...  112 us
  transfers between devices with their start and end apart: 24, of which 19 were waited for; matrix products, arithmetic and copies ran while one was open for 22% of the time, Pallas kernels for 0%

profile of v1, /device:TPU:0, one launch (start us, length us, event | category | flops | bytes accessed | tf_op | source)
XLA Modules:
  0.0 2969.4 jit_solution(7343814497067190750)
XLA Ops:
  37.2 41.9 %all-gather.10.cloned.1.call-done = bf16[1024,1536]{1,0:T(8,128)(2,1)} async-done(((bf16[256,1536]{1,0:T(8,128)(2,1)}), bf16[1024,1536]{1,0:T(8,128)(2,1)}) %all-gather.10.cloned.1.call-update) | async-done | bytes 3145744 | tf_op jit(solution)/shard_map/all_gather | solution.py:187
  89.1 14.5 all-gather.12.cloned.1.call-done
  136.2 110.3 %reduce-scatter.13.cloned.1.call-done = f32[256,1536]{1,0:T(8,128)} async-done(((f32[1024,1536]{1,0:T(8,128)}), f32[256,1536]{1,0:T(8,128)}) %reduce-scatter.13.cloned.1.call-update) | async-done | bytes 1572880 | tf_op jit(solution)/shard_map/reduce_scatter | solution.py:209
  262.8 107.0 %collective-permute-done.1 = bf16[2,10,192,512]{3,2,1,0:T(8,128)(2,1)} collective-permute-done((bf16[2,10,192,512]{3,2,1,0:T(8,128)(2,1)}, bf16[2,10,192,512]{3,2,1,0:T(8,128)(2,1)}, u32[]{:S(2)}, u32[]{:S(2)}) %collective-permute-start.1) | collective-permute-done | bytes 3932192 | tf_op jit(solution)/shard_map/ppermute | solution.py:26
  386.7 268.1 %all-gather = bf16[8,192,40]{1,2,0:T(8,128)(2,1)S(1)} all-gather(bf16[1,192,40]{1,2,0:T(8,128)(2,1)S(1)} %bitcast.441), channel_id=1, replica_groups=mesh['fsdp'=8,'tp'=4] {'fsdp'}, dimensions={0}, use_global_device_ids=true | all-gather | bytes 138240 | tf_op jit(solution)/shard_map/all_gather | solution.py:178
  688.7 466.2 %while.71 = (s32[]{:T(128)}, f32[1024,1536]{1,0:T(8,128)}, s32[10,408]{1,0:T(8,128)}, f32[10,408]{1,0:T(8,128)}, f32[10,408,8]{2,1,0:T(8,128)}, /*index=5*/f32[1...) while((s32[]{:T(128)}, f32[1024,1536]{1,0:T(8,128)}, ...), condition=%wide.region_18.20_spmd, body=%wide.region_10.19_spmd.sunk | while | flops 1929139968 | bytes 35207396 | solution.py:244
  1159.1 504.9 %while.72 = (s32[]{:T(128)}, f32[1024,1536]{1,0:T(8,128)}, f32[1024,8]{1,0:T(8,128)}, f32[10,1536,512]{2,1,0:T(8,128)}, f32[10,1536,512]{2,1,0:T(8,128)}, /*inde...) while((s32[]{:T(128)}, f32[1024,1536]{1,0:T(8,128)}, ...), condition=%wide.region_24.26_spmd, body=%wide.region_20.25_spmd.sunk | while | flops 3863125760 | bytes 57883772 | solution.py:288
  1666.5 18.7 reduce-scatter.19.cloned.1.call-done
  1686.7 109.6 %reduce-scatter.17.cloned.1.call-done = f32[256,1536]{1,0:T(8,128)} async-done(((f32[1024,1536]{1,0:T(8,128)}), f32[256,1536]{1,0:T(8,128)}) %reduce-scatter.17.cloned.1.call-update) | async-done | bytes 1572880 | tf_op jit(solution)/shard_map/reduce_scatter | solution.py:292
  1802.2 63.0 %all-gather.24.cloned.1.call-done = bf16[1024,1536]{1,0:T(8,128)(2,1)} async-done(((bf16[256,1536]{1,0:T(8,128)(2,1)}), bf16[1024,1536]{1,0:T(8,128)(2,1)}) %all-gather.24.cloned.1.call-update) | async-done | bytes 3145744 | tf_op jit(solution)/shard_map/all_gather | solution.py:303
  1870.0 65.1 %while.73 = (s32[]{:T(128)}, f32[2,512,6,64]{1,0,3,2:T(2,128)}, f32[2,512,2,64]{1,0,3,2:T(2,128)}, bf16[2,512,2,64]{1,3,2,0:T(8,128)(2,1)}, bf16[2,512,2,64]{1,3...) while((s32[]{:T(128)}, f32[2,512,6,64]{1,0,3,2:T(2,128)}, ...), condition=%wide.region_32.34_spmd, body=%wide.region_30.33_spmd.sunk | while | flops 1031271424 | bytes 58161316 | solution.py:308
  1887.6 15.0 dynamic_update_slice.116
  1920.1 15.0 dynamic_update_slice.116
  1967.6 26.9 all-reduce.3.cloned.1.call-done
  1996.0 111.9 %reduce-scatter.21.cloned.1.call-done = f32[256,1536]{1,0:T(8,128)} async-done(((f32[1024,1536]{1,0:T(8,128)}), f32[256,1536]{1,0:T(8,128)}) %reduce-scatter.21.cloned.1.call-update) | async-done | bytes 1572880 | tf_op jit(solution)/shard_map/reduce_scatter | solution.py:335
  2109.8 45.1 %all-reduce = (f32[1536]{0:T(1024)}, f32[1536]{0:T(1024)}) all-reduce(f32[1536]{0:T(1024)S(1)} %get-tuple-element.575, f32[1536]{0:T(1024)S(1)} %get-tuple-element.573), channel_id=1, replica_groups=mesh['fsdp'=8,'tp'=4] {'fsdp','tp'}, use_global_device_ids=true, to_apply=%region_36.38 | all-reduce | flops 3072 | bytes 24576 | tf_op jit(solution)/shard_map/psum | solution.py:340
  2154.9 67.5 %reduce-scatter.15.cloned.1.call-done = f32[256,1536]{1,0:T(8,128)} async-done(((f32[1024,1536]{1,0:T(8,128)}), f32[256,1536]{1,0:T(8,128)}) %reduce-scatter.15.cloned.1.call-update) | async-done | bytes 1572880 | tf_op jit(solution)/shard_map/reduce_scatter | solution.py:245
  2227.0 34.4 %reduce-scatter.25.cloned.1.call-done = f32[192,128]{1,0:T(8,128)} async-done(((f32[1536,128]{1,0:T(8,128)}), f32[192,128]{1,0:T(8,128)}) %reduce-scatter.25.cloned.1.call-update) | async-done | bytes 98320 | tf_op jit(solution)/shard_map/reduce_scatter | solution.py:349
  2261.4 38.6 %reduce-scatter.27.cloned.1.call-done = f32[192,128]{1,0:T(8,128)} async-done(((f32[1536,128]{1,0:T(8,128)}), f32[192,128]{1,0:T(8,128)}) %reduce-scatter.27.cloned.1.call-update) | async-done | bytes 98320 | tf_op jit(solution)/shard_map/reduce_scatter | solution.py:350
  2300.0 46.1 %reduce-scatter.29.cloned.1.call-done = f32[192,384]{1,0:T(8,128)} async-done(((f32[1536,384]{1,0:T(8,128)}), f32[192,384]{1,0:T(8,128)}) %reduce-scatter.29.cloned.1.call-update) | async-done | bytes 294928 | tf_op jit(solution)/shard_map/reduce_scatter | solution.py:351
  2346.1 46.2 %reduce-scatter.23.cloned.1.call-done = f32[192,384]{1,0:T(8,128)} async-done(((f32[1536,384]{1,0:T(8,128)}), f32[192,384]{1,0:T(8,128)}) %reduce-scatter.23.cloned.1.call-update) | async-done | bytes 294928 | tf_op jit(solution)/shard_map/reduce_scatter | solution.py:348
  2392.3 190.1 %reduce-scatter.35.cloned.1.call-done = f32[10,192,512]{2,1,0:T(8,128)} async-done(((f32[10,1536,512]{2,1,0:T(8,128)}), f32[10,192,512]{2,1,0:T(8,128)}) %reduce-scatter.35.cloned.1.call-update) | async-done | bytes 3932176 | tf_op jit(solution)/shard_map/reduce_scatter | solution.py:356
  2582.4 189.9 %reduce-scatter.31.cloned.1.call-done = f32[10,192,512]{2,1,0:T(8,128)} async-done(((f32[10,1536,512]{2,1,0:T(8,128)}), f32[10,192,512]{2,1,0:T(8,128)}) %reduce-scatter.31.cloned.1.call-update) | async-done | bytes 3932176 | tf_op jit(solution)/shard_map/reduce_scatter | solution.py:354
  2772.3 190.1 %reduce-scatter.33.cloned.1.call-done = f32[10,192,512]{2,1,0:T(8,128)} async-done(((f32[10,1536,512]{2,1,0:T(8,128)}), f32[10,192,512]{2,1,0:T(8,128)}) %reduce-scatter.33.cloned.1.call-update) | async-done | bytes 3932176 | tf_op jit(solution)/shard_map/reduce_scatter | solution.py:355
  (966 shorter events, 1215.4 us)
Async XLA Ops:
  7.2 72.0 %all-gather.10.cloned.1.call-start = ((), (), s32[]{:S(2)}) async-start(), calls=%async_computation.12 | async-start | bytes 3932160 | tf_op jit(solution)/shard_map/all_gather | solution.py:187
  12.8 90.8 %all-gather.12.cloned.1.call-start = ((), (), s32[]{:S(2)}) async-start(), calls=%async_computation.13 | async-start | bytes 1327104 | tf_op jit(solution)/shard_map/all_gather | solution.py:174
  13.6 115.9 %all-gather.14.cloned.1.call-start = ((), (), s32[]{:S(2)}) async-start(), calls=%async_computation.14 | async-start | bytes 1327104 | tf_op jit(solution)/shard_map/all_gather | solution.py:177
  14.3 232.2 %reduce-scatter.13.cloned.1.call-start = ((), (), s32[]{:S(2)}) async-start(), calls=%async_computation.15 | async-start | bytes 7864320 | tf_op jit(solution)/shard_map/reduce_scatter | solution.py:209
  135.6 549.6 %all-gather.16.cloned.1.call-start = ((), (), s32[]{:S(2)}) async-start(), calls=%async_computation.16 | async-start | bytes 3932160 | tf_op jit(solution)/shard_map/all_gather | solution.py:225
  250.5 434.7 %all-gather.18.cloned.1.call-start = ((), (), s32[]{:S(2)}) async-start(), calls=%async_computation.17 | async-start | bytes 17694720 | tf_op jit(solution)/shard_map/all_gather | solution.py:179
  251.1 434.1 %all-gather.20.cloned.1.call-start = ((), (), s32[]{:S(2)}) async-start(), calls=%async_computation.18 | async-start | bytes 17694720 | tf_op jit(solution)/shard_map/all_gather | solution.py:181
  251.9 903.0 %all-gather.22.cloned.1.call-start = ((), (), s32[]{:S(2)}) async-start(), calls=%async_computation.20 | async-start | bytes 3932160 | tf_op jit(solution)/shard_map/all_gather | solution.py:249
  252.1 4.2 collective-permute-start
  261.5 108.3 %collective-permute-start.1 = (bf16[2,10,192,512]{3,2,1,0:T(8,128)(2,1)}, bf16[2,10,192,512]{3,2,1,0:T(8,128)(2,1)}, u32[]{:S(2)}, u32[]{:S(2)}) collective-permute-start(bf16[2,10,192,512]{3,2,1,0:T(8,128)(2,1)} %pad_maximum_fusion.1), channel_id=1, source_target_pairs={{0,8},{4,12},{8,0},{12,4},{16,24},{20,28},{24,16},{28,20},{1,9},{5... | collective-permute-start | bytes 11796488 | tf_op jit(solution)/shard_map/ppermute | solution.py:26
  384.1 272.0 %collective-permute-start.2 = (bf16[4,10,192,512]{3,2,1,0:T(8,128)(2,1)}, bf16[4,10,192,512]{3,2,1,0:T(8,128)(2,1)}, u32[]{:S(2)}, u32[]{:S(2)}) collective-permute-start(bf16[4,10,192,512]{3,2,1,0:T(8,128)(2,1)} %pad_maximum_fusion), channel_id=1, source_target_pairs={{0,16},{4,20},{8,24},{12,28},{16,0},{20,4},{24,8},{28,12},{1,17},{... | collective-permute-start | bytes 23592968 | tf_op jit(solution)/shard_map/ppermute | solution.py:26
  386.5 1298.7 %reduce-scatter.19.cloned.1.call-start = ((), (), s32[]{:S(2)}) async-start(), calls=%async_computation.22 | async-start | bytes 40960 | tf_op jit(solution)/shard_map/reduce_scatter | solution.py:293
  1665.8 130.5 %reduce-scatter.17.cloned.1.call-start = ((), (), s32[]{:S(2)}) async-start(), calls=%async_computation.21 | async-start | bytes 7864320 | tf_op jit(solution)/shard_map/reduce_scatter | solution.py:292
  1666.4 198.7 %all-gather.24.cloned.1.call-start = ((), (), s32[]{:S(2)}) async-start(), calls=%async_computation.23 | async-start | bytes 3932160 | tf_op jit(solution)/shard_map/all_gather | solution.py:303
  1801.0 193.4 %all-reduce.3.cloned.1.call-start = ((), (), s32[]{:S(2)}) async-start(), calls=%async_computation.29 | async-start | bytes 491520 | tf_op jit(solution)/shard_map/psum | solution.py:340
  1802.1 305.7 %reduce-scatter.21.cloned.1.call-start = ((), (), s32[]{:S(2)}) async-start(), calls=%async_computation.24 | async-start | bytes 7864320 | tf_op jit(solution)/shard_map/reduce_scatter | solution.py:335
  1948.8 273.6 %reduce-scatter.15.cloned.1.call-start = ((), (), s32[]{:S(2)}) async-start(), calls=%async_computation.19 | async-start | bytes 7864320 | tf_op jit(solution)/shard_map/reduce_scatter | solution.py:245
  1949.4 312.0 %reduce-scatter.25.cloned.1.call-start = ((), (), s32[]{:S(2)}) async-start(), calls=%async_computation.26 | async-start | bytes 884736 | tf_op jit(solution)/shard_map/reduce_scatter | solution.py:349
  1952.7 347.3 %reduce-scatter.27.cloned.1.call-start = ((), (), s32[]{:S(2)}) async-start(), calls=%async_computation.27 | async-start | bytes 884736 | tf_op jit(solution)/shard_map/reduce_scatter | solution.py:350
  1955.6 390.5 %reduce-scatter.29.cloned.1.call-start = ((), (), s32[]{:S(2)}) async-start(), calls=%async_computation.28 | async-start | bytes 2654208 | tf_op jit(solution)/shard_map/reduce_scatter | solution.py:351
  1961.0 431.3 %reduce-scatter.23.cloned.1.call-start = ((), (), s32[]{:S(2)}) async-start(), calls=%async_computation.25 | async-start | bytes 2654208 | tf_op jit(solution)/shard_map/reduce_scatter | solution.py:348
  1965.5 616.9 %reduce-scatter.35.cloned.1.call-start = ((), (), s32[]{:S(2)}) async-start(), calls=%async_computation.32 | async-start | bytes 35389440 | tf_op jit(solution)/shard_map/reduce_scatter | solution.py:356
  1966.2 806.0 %reduce-scatter.31.cloned.1.call-start = ((), (), s32[]{:S(2)}) async-start(), calls=%async_computation.30 | async-start | bytes 35389440 | tf_op jit(solution)/shard_map/reduce_scatter | solution.py:354
  1966.8 995.5 %reduce-scatter.33.cloned.1.call-start = ((), (), s32[]{:S(2)}) async-start(), calls=%async_computation.31 | async-start | bytes 35389440 | tf_op jit(solution)/shard_map/reduce_scatter | solution.py:355
  (165 other events, 3400.5 us)
Sparse Core Ops, SparseCore 0:
  12.9 66.1 all-gather.9
  81.0 22.5 all-gather.11
  105.5 23.9 all-gather.13
  135.7 110.7 reduce-scatter.12
  250.7 63.9 all-gather.15
  316.4 136.5 all-gather.17
  454.9 149.6 all-gather.19
  606.2 63.4 all-gather.21
  1666.0 19.2 reduce-scatter.18
  1687.4 108.9 reduce-scatter.16
  1801.2 63.9 all-gather.23
  1870.5 123.9 all-reduce.2
  1996.8 111.0 reduce-scatter.20
  2110.0 112.3 reduce-scatter.14
  2226.0 35.4 reduce-scatter.24
  2265.0 34.9 reduce-scatter.26
  2303.8 42.3 reduce-scatter.28
  2349.9 42.3 reduce-scatter.22
  2396.5 185.8 reduce-scatter.34
  2586.4 185.8 reduce-scatter.30
  2776.5 185.8 reduce-scatter.32
